TPU v7x, 32 devices: a whole 2x2x4 slice. The times are simulated.
32 devices in a mesh: px: 4 (over z), py: 8 (over y, x, core).
Axes of the slice: x: 2, y: 2, z: 4, core: 2. Of those that a mesh axis runs over, the one named last changes fastest.
Arguments:
- features: bfloat16 [24576, 768], P(('px', 'py')), may hold values from -6 to 6
- weight_one: bfloat16 [768, 768], replicated, may hold values from -0.21875 to 0.21875
- weight_two: bfloat16 [768, 768], replicated, may hold values from -0.21875 to 0.21875
- tile_values: bfloat16 [1024, 128, 128], P(('px', 'py')), may hold values from -0.375 to 0.375
- tile_rows: int32 [32, 32], P(('px', 'py')), may hold values from 0 to 5
- tile_cols: int32 [32, 32], P(('px', 'py')), may hold values from 0 to 7
- tile_count: int32 [32], P(('px', 'py')), may hold values from 4 to 32, as said below
- send_rows: int32 [32, 32, 8], P(('px', 'py')), may hold values from 0 to 767
- send_count: int32 [32, 32], P(('px', 'py')), may hold values from 1 to 8, as said below
- stale_hidden: bfloat16 [8192, 768], P(('px', 'py')), may hold values from -3 to 3
- stale_grad: bfloat16 [8192, 768], P(('px', 'py')), may hold values from -6 to 6
- out_grad: bfloat16 [24576, 768], P(('px', 'py')), may hold values from -6 to 6
Outputs:
- next_hidden: bfloat16 [8192, 768], P(('px', 'py'))
- next_grad: bfloat16 [8192, 768], P(('px', 'py'))
- grad_one: float32 [768, 768], replicated
- grad_two: float32 [768, 768], replicated
Inputs may be any that keep to these rules, and one draw needn't show every extreme that they name: The tiles of a part with index below its tile_count are live, the others are ignored; some part has 32 live tiles in every draw. `tile_cols`: column tiles below 6 hold the part's own rows; the rest hold the received boundary rows, 8 slots from each part in order of the part. `send_rows`: slots at or beyond the matching send_count are unused. `send_count`: every part sends 8 rows to at least one peer in every draw.
All inputs are finite; a program needn't handle non-finite values.
Results may differ from a plain program's by a relative error of at most 0.0061.
Values may be sent and summed in bfloat16 or wider, within the bound.
A program may use at most 128 MiB of HBM per device.

v0:
```python
import functools
import math

import jax
import jax.numpy as jnp
from jax import lax
from jax.experimental import pallas as pl
from jax.experimental.pallas import tpu as pltpu
from jax.sharding import PartitionSpec as P

MESH = pl.DeviceIdType.MESH
BF16 = jnp.bfloat16
F32 = jnp.float32


def split_axis(size):
    out, stride = [], 1
    while size > 1:
        two = size & (size - 1) == 0
        step = size if not two else (2 if (size.bit_length() - 1) % 2 else 4)
        out.append((stride, step))
        stride *= step
        size //= step
    return out


def positions(npx, npy):
    px, py = lax.axis_index("px"), lax.axis_index("py")
    return px, py, px * npy + py


def entry_barrier(me, npx, npy):
    parts = npx * npy
    barrier = pltpu.get_barrier_semaphore()

    def greet(step, carry):
        peer = lax.rem(me + step, parts)
        pl.semaphore_signal(
            barrier, inc=1, device_id=(peer // npy, lax.rem(peer, npy)), device_id_type=MESH
        )
        return carry

    lax.fori_loop(1, parts, greet, 0)
    pl.semaphore_wait(barrier, parts - 1)


def start_exchange(me, npx, npy, pairs, send_sem, recv_sem):
    parts = npx * npy

    def send(step, carry):
        peer = lax.rem(me + step, parts)
        for k, (src, dst) in enumerate(pairs):
            pltpu.make_async_remote_copy(
                src_ref=src.at[peer],
                dst_ref=dst.at[me],
                send_sem=send_sem.at[k],
                recv_sem=recv_sem.at[k],
                device_id=(peer // npy, lax.rem(peer, npy)),
                device_id_type=MESH,
            ).start()
        return carry

    lax.fori_loop(1, parts, send, 0)
    for src, dst in pairs:
        dst[me] = src[me]


def finish_exchange(parts, pairs, send_sem, recv_sem):
    for k, (src, dst) in enumerate(pairs):
        part_of = dst.at[pl.ds(0, parts - 1)]
        pltpu.make_async_copy(part_of, part_of, recv_sem.at[k]).wait()
        part_of = src.at[pl.ds(0, parts - 1)]
        pltpu.make_async_copy(part_of, part_of, send_sem.at[k]).wait()


def exchange_kernel(npx, npy, count, *refs):
    srcs, dsts = refs[:count], refs[count : 2 * count]
    send_sem, recv_sem = refs[2 * count :]
    px, py, me = positions(npx, npy)
    entry_barrier(me, npx, npy)
    pairs = list(zip(srcs, dsts))
    start_exchange(me, npx, npy, pairs, send_sem, recv_sem)
    finish_exchange(npx * npy, pairs, send_sem, recv_sem)


def exchange(npx, npy, arrays, collective_id):
    vmem = pl.BlockSpec(memory_space=pltpu.VMEM)
    n = len(arrays)
    return pl.pallas_call(
        functools.partial(exchange_kernel, npx, npy, n),
        out_shape=tuple(jax.ShapeDtypeStruct(a.shape, a.dtype) for a in arrays),
        in_specs=[vmem] * n,
        out_specs=(vmem,) * n,
        scratch_shapes=[pltpu.SemaphoreType.DMA((n,)), pltpu.SemaphoreType.DMA((n,))],
        compiler_params=pltpu.CompilerParams(
            collective_id=collective_id, has_side_effects=True, vmem_limit_bytes=40 * 2**20
        ),
        name="exchange",
    )(*arrays)


def reduce_orders(npx, npy):
    dims = [("py", s, k) for s, k in split_axis(npy)] + [("px", s, k) for s, k in split_axis(npx)]
    near = [d for d in dims if d[2] == 2]
    far = [d for d in dims if d[2] != 2]
    return [near + far, near + far[::-1]]


class Stream:
    def __init__(self, order, parts, px, py, src, out, curs, recvs, sems):
        self.order, self.src, self.out, self.curs, self.recvs = order, src, out, curs, recvs
        self.send_sem, self.recv_sem, self.at = sems
        self.px, self.py = px, py
        self.coord, self.span, left = [], [], parts
        for axis, stride, size in order:
            index = px if axis == "px" else py
            self.coord.append(lax.rem(index // stride, size))
            left //= size
            self.span.append(left)
        self.base, total = [], 0
        for c, n in zip(self.coord, self.span):
            total = total + c * n
            self.base.append(total)
        self.live = {}

    def peer(self, stage, offset):
        axis, stride, size = self.order[stage]
        mine = self.coord[stage]
        other = lax.rem(mine + offset, size)
        move = (other - mine) * stride
        where = (self.px + move, self.py) if axis == "px" else (self.px, self.py + move)
        return other, where

    def copies(self, key, stage, make):
        made = []
        for offset in range(1, self.order[stage][2]):
            other, where = self.peer(stage, offset)
            src, dst = make(offset, other)
            copy = pltpu.make_async_remote_copy(
                src_ref=src,
                dst_ref=dst,
                send_sem=self.send_sem.at[self.at],
                recv_sem=self.recv_sem.at[self.at],
                device_id=where,
                device_id_type=MESH,
            )
            self.at += 1
            copy.start()
            made.append(copy)
        self.live[key] = made

    def scatter_start(self, stage):
        n = self.span[stage]
        cur = self.src if stage == 0 else self.curs[stage - 1]
        self.copies(
            ("rs", stage),
            stage,
            lambda offset, other: (cur.at[pl.ds(other * n, n)], self.recvs[stage].at[offset - 1]),
        )

    def scatter_finish(self, stage):
        n = self.span[stage]
        cur = self.src if stage == 0 else self.curs[stage - 1]
        last = stage == len(self.order) - 1
        target = self.out if last else self.curs[stage]
        start = self.base[stage] if last else 0
        for copy in self.live[("rs", stage)]:
            copy.wait_recv()
        mine = self.coord[stage] * n
        size = self.order[stage][2]

        def add(i, carry):
            total = cur[mine + i].astype(F32)
            for offset in range(1, size):
                total = total + self.recvs[stage][offset - 1, i].astype(F32)
            target[start + i] = total.astype(BF16)
            return carry

        lax.fori_loop(0, n, add, 0)

    def gather_start(self, stage):
        n = self.span[stage]
        block = self.out.at[pl.ds(self.base[stage], n)]
        self.copies(("ag", stage), stage, lambda offset, other: (block, block))

    def gather_finish(self, stage):
        for copy in self.live[("ag", stage)]:
            copy.wait_recv()

    def drain(self):
        for made in self.live.values():
            for copy in made:
                copy.wait_send()


def scratch_for(order, parts, height, width):
    curs, recvs, left = [], [], parts
    for stage, (_, _, size) in enumerate(order):
        left //= size
        recvs.append(pltpu.VMEM((size - 1, left, height, width), BF16))
        if stage < len(order) - 1:
            curs.append(pltpu.VMEM((left, height, width), BF16))
    return curs, recvs


def sum_kernel(npx, npy, box, part_one, part_two, got, out_one, out_two, *scratch):
    parts = npx * npy
    px, py, me = positions(npx, npy)
    orders = reduce_orders(npx, npy)
    stages = len(orders[0])
    box_send, box_recv, red_send, red_recv = scratch[-4:]
    per = 2 * sum(size - 1 for _, _, size in orders[0])
    streams, at = [], 0
    for k, (order, src, out) in enumerate(zip(orders, (part_one, part_two), (out_one, out_two))):
        curs = scratch[at : at + stages - 1]
        recvs = scratch[at + stages - 1 : at + 2 * stages - 1]
        at += 2 * stages - 1
        streams.append(
            Stream(order, parts, px, py, src, out, curs, recvs, (red_send, red_recv, k * per))
        )
    entry_barrier(me, npx, npy)
    for s in streams:
        s.scatter_start(0)
    start_exchange(me, npx, npy, [(box, got)], box_send, box_recv)
    for stage in range(stages):
        for s in streams:
            s.scatter_finish(stage)
            if stage < stages - 1:
                s.scatter_start(stage + 1)
            else:
                s.gather_start(stage)
    for stage in range(stages - 1, -1, -1):
        for s in streams:
            s.gather_finish(stage)
            if stage > 0:
                s.gather_start(stage - 1)
    finish_exchange(parts, [(box, got)], box_send, box_recv)
    for s in streams:
        s.drain()


def sum_and_exchange(npx, npy, box, part_one, part_two, collective_id):
    parts = npx * npy
    vmem = pl.BlockSpec(memory_space=pltpu.VMEM)
    _, height, width = part_one.shape
    orders = reduce_orders(npx, npy)
    scratch = []
    for order in orders:
        curs, recvs = scratch_for(order, parts, height, width)
        scratch += curs + recvs
    count = 2 * 2 * sum(size - 1 for _, _, size in orders[0])
    dma = pltpu.SemaphoreType.DMA
    return pl.pallas_call(
        functools.partial(sum_kernel, npx, npy),
        out_shape=tuple(
            jax.ShapeDtypeStruct(a.shape, a.dtype) for a in (box, part_one, part_two)
        ),
        in_specs=[vmem] * 3,
        out_specs=(vmem,) * 3,
        scratch_shapes=scratch + [dma((1,)), dma((1,)), dma((count,)), dma((count,))],
        compiler_params=pltpu.CompilerParams(
            collective_id=collective_id, has_side_effects=True, vmem_limit_bytes=56 * 2**20
        ),
        name="sum_and_exchange",
    )(box, part_one, part_two)


def dense_kernel(rows, cols, live, tiles, own, rest, total):
    row_tiles, col_tiles, tile, _ = total.shape
    total[...] = jnp.zeros_like(total)

    def add(t, carry):
        r, c = rows[0, t], cols[0, t]
        total[r, c] += tiles[t].astype(F32)
        return carry

    lax.fori_loop(0, live[0], add, 0)
    for r in range(row_tiles):
        for c in range(col_tiles):
            out, at = (own, c) if c < row_tiles else (rest, c - row_tiles)
            out[r * tile : (r + 1) * tile, at * tile : (at + 1) * tile] = total[r, c].astype(BF16)


def dense_tiles(tile_values, tile_rows, tile_cols, tile_count, row_tiles, col_tiles):
    tile = tile_values.shape[1]
    vmem = pl.BlockSpec(memory_space=pltpu.VMEM)
    smem = pl.BlockSpec(memory_space=pltpu.SMEM)
    rows = row_tiles * tile
    return pl.pallas_call(
        dense_kernel,
        out_shape=(
            jax.ShapeDtypeStruct((rows, rows), BF16),
            jax.ShapeDtypeStruct((rows, (col_tiles - row_tiles) * tile), BF16),
        ),
        in_specs=[smem, smem, smem, vmem],
        out_specs=(vmem, vmem),
        scratch_shapes=[pltpu.VMEM((row_tiles, col_tiles, tile, tile), F32)],
        compiler_params=pltpu.CompilerParams(vmem_limit_bytes=32 * 2**20),
        name="dense_tiles",
    )(tile_rows, tile_cols, tile_count, tile_values)


def dot(a, b, ca=1, cb=0):
    return lax.dot_general(a, b, (((ca,), (cb,)), ((), ())), preferred_element_type=F32)


def local(
    npx,
    npy,
    features,
    weight_one,
    weight_two,
    tile_values,
    tile_rows,
    tile_cols,
    tile_count,
    send_rows,
    send_count,
    stale_hidden,
    stale_grad,
    out_grad,
):
    parts = npx * npy
    rows_own, width = features.shape
    slots = send_rows.shape[2]
    tile = tile_values.shape[1]
    row_tiles = rows_own // tile
    col_tiles = (rows_own + parts * slots) // tile
    counts = send_count[0]
    slot_ids = jnp.arange(slots, dtype=jnp.int32)
    sent = (slot_ids[None, :] < counts[:, None]).reshape(-1)
    chosen = jnp.where(sent, send_rows[0].reshape(-1), -1)
    pick = (chosen[:, None] == jnp.arange(rows_own, dtype=jnp.int32)[None, :]).astype(BF16)
    own, rest = dense_tiles(tile_values, tile_rows, tile_cols, tile_count, row_tiles, col_tiles)

    down = dot(out_grad, weight_two, 1, 1).astype(BF16)
    box_g = dot(rest, down, 0, 0).astype(BF16)
    box_x = dot(pick, features).astype(BF16)
    box_n = jnp.broadcast_to(counts[:, None, None], (parts, 1, 128))
    in_x, in_g, in_n = exchange(
        npx,
        npy,
        (box_x.reshape(parts, slots, width), box_g.reshape(parts, slots, width), box_n),
        0,
    )
    heard = slot_ids[None, :] < in_n[:, 0, :1]
    agg_one = (dot(own, features) + dot(rest, in_x.reshape(-1, width))).astype(BF16)
    pre_one = dot(agg_one, weight_one)
    cdf = 0.5 * (1.0 + lax.erf(pre_one * (1.0 / math.sqrt(2.0))))
    hidden = (pre_one * cdf).astype(BF16)
    slope = cdf + pre_one * (jnp.exp(-0.5 * pre_one * pre_one) * (1.0 / math.sqrt(2.0 * math.pi)))
    box_h = dot(pick, hidden).astype(BF16)
    kept = jnp.where(heard.reshape(-1, 1), stale_hidden, jnp.zeros_like(stale_hidden))
    agg_two = (dot(own, hidden) + dot(rest, kept)).astype(BF16)
    hidden_grad = dot(own, down, 0, 0) + dot(pick, stale_grad, 0, 0)
    pre_grad = (hidden_grad * slope).astype(BF16)
    part_one = dot(agg_one, pre_grad, 0, 0).astype(BF16)
    part_two = dot(agg_two, out_grad, 0, 0).astype(BF16)

    height = -(-width // (8 * parts)) * 8
    pad = height * parts - width

    def cut(a):
        return jnp.pad(a, ((0, pad), (0, 0))).reshape(parts, height, width)

    got, sum_one, sum_two = sum_and_exchange(
        npx, npy, box_h.reshape(parts, slots, width), cut(part_one), cut(part_two), 1
    )
    scale = 1.0 / math.sqrt(rows_own * parts)

    def whole(a):
        return a.reshape(-1, width)[:width].astype(F32) * scale

    in_g = in_g.reshape(-1, width)
    next_grad = jnp.where(sent[:, None], in_g, jnp.zeros_like(in_g))
    return got.reshape(-1, width), next_grad, whole(sum_one), whole(sum_two)


def solution(mesh):
    in_specs = (
        P(("px", "py"), None),
        P(),
        P(),
        P(("px", "py"), None, None),
        P(("px", "py"), None),
        P(("px", "py"), None),
        P(("px", "py")),
        P(("px", "py"), None, None),
        P(("px", "py"), None),
        P(("px", "py"), None),
        P(("px", "py"), None),
        P(("px", "py"), None),
    )
    out_specs = (P(("px", "py"), None), P(("px", "py"), None), P(), P())
    body = functools.partial(local, mesh.shape["px"], mesh.shape["py"])
    return jax.shard_map(body, mesh=mesh, in_specs=in_specs, out_specs=out_specs, check_vma=False)
```

profile of v0, /device:TPU:0, one launch (start us, length us, event | category | flops | bytes accessed | tf_op | source)
XLA Modules:
  0.0 118.6 jit_solution(11781695404054959559)
XLA Ops:
  0.6 0.0 copy-start
  0.6 0.0 copy-start.7
  1.5 0.7 iota_compare_fusion.6
  2.2 0.1 lt.52
  2.3 0.8 copy.16
  3.0 0.1 reshape_squeeze.3
  3.1 0.7 broadcast_in_dim.27.refs_2_
  3.9 1.8 %fusion.6.refs_0_ = bf16[32,8,768]{2,1,0:T(8,128)(2,1)S(1)} fusion(bf16[768,768]{1,0:T(8,128)(2,1)} %param.12, s32[256]{0:T(256)S(1)} %broadcast_select_fusion), kind=kOutput, calls=%fused_computation.19 | convolution fusion | flops 302383104 | bytes 1573888 | tf_op jit(solution)/shard_map/dot_general | solution.py:304
  5.7 0.0 copy-done.7
  5.7 0.0 copy-start.1
  5.7 0.0 copy-start.2
  5.7 0.0 copy-start.3
  5.7 2.5 %convolution_convert_fusion.2 = bf16[768,768]{1,0:T(8,128)(2,1)S(1)} fusion(bf16[768,768]{1,0:T(8,128)(2,1)} %param.23, bf16[768,768]{1,0:T(8,128)(2,1)S(1)} %copy-done.7), kind=kOutput, calls=%fused_computation.15 | convolution fusion | flops 906559488 | bytes 3538944 | tf_op jit(solution)/shard_map/dot_general | solution.py:304
  8.2 0.0 copy-done.1
  8.2 0.0 copy-done.2
  8.2 0.0 copy-done.3
  8.3 0.0 copy-start.4
  8.3 1.1 dense_tiles.1
  9.3 0.0 copy-done.4
  9.4 0.5 fusion.7.refs_1_
  9.9 20.6 %exchange.1 = (bf16[32,8,768]{2,1,0:T(8,128)(2,1)S(1)}, bf16[32,8,768]{2,1,0:T(8,128)(2,1)S(1)}, s32[32,1,128]{2,1,0:T(1,128)S(1)}) custom-call(bf16[32,8,768]{2,1,0:T(8,128)(2,1)S(1)} %fusion.6.refs_0_, bf16[32,8,768]{2,1,0:T(8,128)(2,1)S(1)} %fusion.7.refs_1_, s32[32,1,128]{2,1,0:T(1,128)S(1)} %broadcast_in_dim.27.refs_2_), custom_call_target="tpu_custom_call" | custom-call | tf_op jit(solution)/shard_map/exchange/pallas_call | solution.py:89
  30.4 0.7 slice_reduce_fusion
  31.1 0.1 iota_compare_fusion.5
  31.2 0.1 lt.57
  31.3 0.9 bitcast_select_fusion
  32.1 0.0 copy-start.8
  32.2 3.9 %fusion.25 = f32[768,768]{1,0:T(8,128)} fusion(bf16[768,768]{1,0:T(8,128)(2,1)S(1)} %get-tuple-element.12, bf16[768,768]{1,0:T(8,128)(2,1)} %copy-done.4), kind=kOutput, calls=%fused_computation.39 | convolution fusion | flops 905969664 | bytes 4718592 | tf_op jit(solution)/shard_map/dot_general | solution.py:304
  36.0 0.0 copy-done.8
  36.0 1.1 fusion.24
  37.1 0.5 add_convert_fusion.1
  37.6 0.0 copy-done
  37.6 0.0 copy-start.5
  37.6 0.0 copy-start.9
  37.7 2.9 %multiply_convert_fusion = (bf16[768,768]{1,0:T(8,128)(2,1)}, f32[768,768]{1,0:T(8,128)}) fusion(bf16[768,768]{1,0:T(8,128)(2,1)S(1)} %add_convert_fusion.1, bf16[768,768]{1,0:T(8,128)(2,1)S(1)} %copy-done), kind=kOutput, calls=%fused_computation.10 | convolution fusion | flops 908918784 | bytes 5898240 | tf_op jit(solution)/shard_map/dot_general | solution.py:304
  40.6 0.0 copy-done.5
  40.6 0.0 copy-done.9
  40.6 5.9 %convolution_convert_fusion.1 = bf16[768,768]{1,0:T(8,128)(2,1)} fusion(bf16[768,768]{1,0:T(8,128)(2,1)} %copy-done.5, f32[768,768]{1,0:T(8,128)} %get-tuple-element.21, f32[768,768]{1,0:T(8,128)} %fusion.25, bf16[256,768]{1,0:T(8,128)(2,1)S(1)} %copy-done.9, s32[256]{0:T(256)S(1)} %broadcast_select_fusion), kind=kOutput, calls=%fused_computation.14 | convolution fusion | flops 1215234048 | bytes 7472128 | tf_op jit(solution)/shard_map/dot_general | solution.py:304
  46.5 0.0 copy-start.11
  46.5 2.6 %fusion.8.box = bf16[32,8,768]{2,1,0:T(8,128)(2,1)} fusion(bf16[768,768]{1,0:T(8,128)(2,1)} %get-tuple-element.20, s32[256]{0:T(256)S(1)} %broadcast_select_fusion), kind=kOutput, calls=%fused_computation.21 | convolution fusion | flops 302383104 | bytes 1573888 | tf_op jit(solution)/shard_map/dot_general | solution.py:304
  49.1 0.0 copy-done.11
  49.1 0.0 copy-start.10
  49.1 2.5 %fusion.26 = f32[768,768]{1,0:T(8,128)} fusion(bf16[768,768]{1,0:T(8,128)(2,1)S(1)} %get-tuple-element.12, bf16[768,768]{1,0:T(8,128)(2,1)S(1)} %copy-done.11), kind=kOutput, calls=%fused_computation.40 | convolution fusion | flops 905969664 | bytes 4718592 | tf_op jit(solution)/shard_map/dot_general | solution.py:304
  51.6 0.0 copy-done.10
  51.6 5.0 %convolution_convert_fusion = bf16[768,768]{1,0:T(8,128)(2,1)} fusion(bf16[768,768]{1,0:T(8,128)(2,1)} %param.23, f32[768,768]{1,0:T(8,128)} %fusion.26, bf16[768,256]{1,0:T(8,128)(2,1)S(1)} %get-tuple-element.13, bf16[256,768]{1,0:T(8,128)(2,1)S(1)} %copy-done.10, pred[256]{0:T(512)(128)(4,1)S(1)} %lt.57), kind=kOutput, calls=%fused_computation.13 | convolution fusion | flops 1209925632 | bytes 5505280 | tf_op jit(solution)/shard_map/dot_general | solution.py:304
  56.6 56.9 %sum_and_exchange.1 = (bf16[32,8,768]{2,1,0:T(8,128)(2,1)}, bf16[32,24,768]{2,1,0:T(8,128)(2,1)}, bf16[32,24,768]{2,1,0:T(8,128)(2,1)}) custom-call(bf16[32,8,768]{2,1,0:T(8,128)(2,1)} %fusion.8.box, bf16[32,24,768]{2,1,0:T(8,128)(2,1)} %bitcast.38, bf16[32,24,768]{2,1,0:T(8,128)(2,1)} %bitcast.39), custom_call_target="tpu_custom_call" | custom-call | tf_op jit(solution)/shard_map/sum_and_exchange/pallas_call | solution.py:253
  113.5 0.0 copy-start.6
  113.5 4.3 %convert_multiply_fusion = (f32[32,24,768]{2,1,0:T(8,128)}, f32[32,24,768]{2,1,0:T(8,128)}) fusion(bf16[32,24,768]{2,1,0:T(8,128)(2,1)} %get-tuple-element.19, bf16[32,24,768]{2,1,0:T(8,128)(2,1)} %get-tuple-element.18), kind=kLoop, calls=%fused_computation.7 | loop fusion | flops 2359296 | bytes 7077888 | tf_op jit(solution)/shard_map/mul | solution.py:372
  117.8 0.0 copy-done.6
  117.8 0.7 copy.19
  (1 shorter events, 0.0 us)
Async XLA Ops:
  0.6 37.0 %copy-start = (bf16[768,768]{1,0:T(8,128)(2,1)S(1)}, bf16[768,768]{1,0:T(8,128)(2,1)}, u32[]{:S(2)}) copy-start(bf16[768,768]{1,0:T(8,128)(2,1)} %param.13) | copy-start | bytes 3538948
  0.6 5.1 %copy-start.7 = (bf16[768,768]{1,0:T(8,128)(2,1)S(1)}, bf16[768,768]{1,0:T(8,128)(2,1)}, u32[]{:S(2)}) copy-start(bf16[768,768]{1,0:T(8,128)(2,1)} %param.14) | copy-start | bytes 3538948
  5.7 2.5 %copy-start.1 = (bf16[32,128,128]{2,1,0:T(8,128)(2,1)S(1)}, bf16[32,128,128]{2,1,0:T(8,128)(2,1)}, u32[]{:S(2)}) copy-start(bf16[32,128,128]{2,1,0:T(8,128)(2,1)} %tiles.1) | copy-start | bytes 3145732
  5.7 2.5 %copy-start.2 = (s32[1,32]{1,0:T(1,128)S(1)}, s32[1,32]{1,0:T(1,128)}, u32[]{:S(2)}) copy-start(s32[1,32]{1,0:T(1,128)} %rows.1) | copy-start | bytes 388
  5.7 2.5 %copy-start.3 = (s32[1,32]{1,0:T(1,128)S(1)}, s32[1,32]{1,0:T(1,128)}, u32[]{:S(2)}) copy-start(s32[1,32]{1,0:T(1,128)} %cols.1) | copy-start | bytes 388
  8.3 1.1 copy-start.4
  32.1 3.9 %copy-start.8 = (bf16[768,768]{1,0:T(8,128)(2,1)S(1)}, bf16[768,768]{1,0:T(8,128)(2,1)}, u32[]{:S(2)}) copy-start(bf16[768,768]{1,0:T(8,128)(2,1)} %param.12) | copy-start | bytes 3538948
  37.6 2.9 %copy-start.5 = (bf16[768,768]{1,0:T(8,128)(2,1)}, bf16[768,768]{1,0:T(8,128)(2,1)S(1)}, u32[]{:S(2)}) copy-start(bf16[768,768]{1,0:T(8,128)(2,1)S(1)} %add_convert_fusion.1) | copy-start | bytes 3538948
  37.6 2.9 %copy-start.9 = (bf16[256,768]{1,0:T(8,128)(2,1)S(1)}, bf16[256,768]{1,0:T(8,128)(2,1)}, u32[]{:S(2)}) copy-start(bf16[256,768]{1,0:T(8,128)(2,1)} %param.22) | copy-start | bytes 1179652
  46.5 2.6 %copy-start.11 = (bf16[768,768]{1,0:T(8,128)(2,1)S(1)}, bf16[768,768]{1,0:T(8,128)(2,1)}, u32[]{:S(2)}) copy-start(bf16[768,768]{1,0:T(8,128)(2,1)} %get-tuple-element.20) | copy-start | bytes 3538948
  49.1 2.5 %copy-start.10 = (bf16[256,768]{1,0:T(8,128)(2,1)S(1)}, bf16[256,768]{1,0:T(8,128)(2,1)}, u32[]{:S(2)}) copy-start(bf16[256,768]{1,0:T(8,128)(2,1)} %param.21) | copy-start | bytes 1179652
  113.5 4.3 %copy-start.6 = (bf16[32,8,768]{2,1,0:T(8,128)(2,1)S(1)}, bf16[32,8,768]{2,1,0:T(8,128)(2,1)}, u32[]{:S(2)}) copy-start(bf16[32,8,768]{2,1,0:T(8,128)(2,1)} %get-tuple-element.16) | copy-start | bytes 1179652
where the time goes:
time: 119 us
  Pallas kernels  78.5 us (66%)
  matrix products  29.2 us (25%)
  other arithmetic  5.95 us (5%)
  local copies, waits for them, and re-layouts  3.29 us (3%)
  between operations  1.63 us (1%)
    pallas_call x1, Pallas kernels, sum_and_exchange(): pl.pallas_call(functools.partial(sum_kernel, npx, npy), out_shape=tuple((...  56.9 us
    dot_general x11, matrix products, dot(): lax.dot_general(a, b, (((ca,), (cb,)), ((), ())), preferred_element_type=...  29.2 us
    pallas_call x1, Pallas kernels, exchange(): pl.pallas_call(functools.partial(exchange_kernel, npx, npy, n), out_shape...  20.6 us
    mul x1, other arithmetic, whole(): return a.reshape(-1, width)[:width].astype(F32) * scale  4.28 us

commit v1 on v0

v1 whole, which is shorter than its diff:
```python
import functools
import math

import jax
import jax.numpy as jnp
from jax import lax
from jax.experimental import pallas as pl
from jax.experimental.pallas import tpu as pltpu
from jax.sharding import PartitionSpec as P

MESH = pl.DeviceIdType.MESH
BF16 = jnp.bfloat16
F32 = jnp.float32


def split_axis(size):
    out, stride = [], 1
    while size > 1:
        two = size & (size - 1) == 0
        step = size if not two else (2 if (size.bit_length() - 1) % 2 else 4)
        out.append((stride, step))
        stride *= step
        size //= step
    return out


def positions(npx, npy):
    px, py = lax.axis_index("px"), lax.axis_index("py")
    return px, py, px * npy + py


def entry_barrier(me, npx, npy):
    parts = npx * npy
    barrier = pltpu.get_barrier_semaphore()

    def greet(step, carry):
        peer = lax.rem(me + step, parts)
        pl.semaphore_signal(
            barrier, inc=1, device_id=(peer // npy, lax.rem(peer, npy)), device_id_type=MESH
        )
        return carry

    lax.fori_loop(1, parts, greet, 0)
    pl.semaphore_wait(barrier, parts - 1)


def start_exchange(me, npx, npy, pairs, send_sem, recv_sem):
    parts = npx * npy

    def send(step, carry):
        peer = lax.rem(me + step, parts)
        for k, (src, dst) in enumerate(pairs):
            pltpu.make_async_remote_copy(
                src_ref=src.at[peer],
                dst_ref=dst.at[me],
                send_sem=send_sem.at[k],
                recv_sem=recv_sem.at[k],
                device_id=(peer // npy, lax.rem(peer, npy)),
                device_id_type=MESH,
            ).start()
        return carry

    lax.fori_loop(1, parts, send, 0)
    for src, dst in pairs:
        dst[me] = src[me]


def finish_exchange(parts, pairs, send_sem, recv_sem):
    for k, (src, dst) in enumerate(pairs):
        part_of = dst.at[pl.ds(0, parts - 1)]
        pltpu.make_async_copy(part_of, part_of, recv_sem.at[k]).wait()
        part_of = src.at[pl.ds(0, parts - 1)]
        pltpu.make_async_copy(part_of, part_of, send_sem.at[k]).wait()


def reduce_orders(npx, npy):
    dims = [("py", s, k) for s, k in split_axis(npy)] + [("px", s, k) for s, k in split_axis(npx)]
    near = [d for d in dims if d[2] == 2]
    far = [d for d in dims if d[2] != 2]
    return [near + far, near + far[::-1]]


class Stream:
    def __init__(self, order, parts, px, py, src, out, curs, recvs, sems):
        self.order, self.src, self.out, self.curs, self.recvs = order, src, out, curs, recvs
        self.send_sem, self.recv_sem, self.at = sems
        self.px, self.py = px, py
        self.coord, self.span, left = [], [], parts
        for axis, stride, size in order:
            index = px if axis == "px" else py
            self.coord.append(lax.rem(index // stride, size))
            left //= size
            self.span.append(left)
        self.base, total = [], 0
        for c, n in zip(self.coord, self.span):
            total = total + c * n
            self.base.append(total)
        self.live = {}

    def peer(self, stage, offset):
        axis, stride, size = self.order[stage]
        mine = self.coord[stage]
        other = lax.rem(mine + offset, size)
        move = (other - mine) * stride
        where = (self.px + move, self.py) if axis == "px" else (self.px, self.py + move)
        return other, where

    def copies(self, key, stage, make):
        made = []
        for offset in range(1, self.order[stage][2]):
            other, where = self.peer(stage, offset)
            src, dst = make(offset, other)
            copy = pltpu.make_async_remote_copy(
                src_ref=src,
                dst_ref=dst,
                send_sem=self.send_sem.at[self.at],
                recv_sem=self.recv_sem.at[self.at],
                device_id=where,
                device_id_type=MESH,
            )
            self.at += 1
            copy.start()
            made.append(copy)
        self.live[key] = made

    def scatter_start(self, stage):
        n = self.span[stage]
        cur = self.src if stage == 0 else self.curs[stage - 1]
        self.copies(
            ("rs", stage),
            stage,
            lambda offset, other: (cur.at[pl.ds(other * n, n)], self.recvs[stage].at[offset - 1]),
        )

    def scatter_finish(self, stage):
        n = self.span[stage]
        cur = self.src if stage == 0 else self.curs[stage - 1]
        last = stage == len(self.order) - 1
        target = self.out if last else self.curs[stage]
        start = self.base[stage] if last else 0
        for copy in self.live[("rs", stage)]:
            copy.wait_recv()
        mine = self.coord[stage] * n
        size = self.order[stage][2]

        def add(i, carry):
            total = cur[mine + i].astype(F32)
            for offset in range(1, size):
                total = total + self.recvs[stage][offset - 1, i].astype(F32)
            target[start + i] = total.astype(BF16)
            return carry

        lax.fori_loop(0, n, add, 0)

    def gather_start(self, stage):
        n = self.span[stage]
        block = self.out.at[pl.ds(self.base[stage], n)]
        self.copies(("ag", stage), stage, lambda offset, other: (block, block))

    def gather_finish(self, stage):
        for copy in self.live[("ag", stage)]:
            copy.wait_recv()

    def drain(self):
        for made in self.live.values():
            for copy in made:
                copy.wait_send()


def scratch_for(order, parts, height, width):
    curs, recvs, left = [], [], parts
    for stage, (_, _, size) in enumerate(order):
        left //= size
        recvs.append(pltpu.VMEM((size - 1, left, height, width), BF16))
        if stage < len(order) - 1:
            curs.append(pltpu.VMEM((left, height, width), BF16))
    return curs, recvs


def dot(a, b, ca=1, cb=0):
    return lax.dot_general(a, b, (((ca,), (cb,)), ((), ())), preferred_element_type=F32)


def dense_kernel(rows, cols, live, tiles, chosen, features, own, rest, pick, box, total):
    row_tiles, col_tiles, tile, _ = total.shape
    slots = box.shape[1]
    node = lax.broadcasted_iota(jnp.int32, pick.shape, 0)
    pick[...] = (node == chosen[...]).astype(F32).astype(BF16)
    out = dot(pick[...], features[...], 0, 0)
    box[...] = out.reshape(-1, slots, out.shape[1]).astype(BF16)
    total[...] = jnp.zeros_like(total)

    def add(t, carry):
        r, c = rows[0, t], cols[0, t]
        total[r, c] += tiles[t].astype(F32)
        return carry

    lax.fori_loop(0, live[0], add, 0)
    for r in range(row_tiles):
        for c in range(col_tiles):
            out, at = (own, c) if c < row_tiles else (rest, c - row_tiles)
            out[r * tile : (r + 1) * tile, at * tile : (at + 1) * tile] = total[r, c].astype(BF16)


def dense_tiles(tile_values, tile_rows, tile_cols, tile_count, chosen, features, parts):
    tile = tile_values.shape[1]
    rows, width = features.shape
    boundary = chosen.shape[1]
    vmem = pl.BlockSpec(memory_space=pltpu.VMEM)
    smem = pl.BlockSpec(memory_space=pltpu.SMEM)
    return pl.pallas_call(
        dense_kernel,
        out_shape=(
            jax.ShapeDtypeStruct((rows, rows), BF16),
            jax.ShapeDtypeStruct((rows, boundary), BF16),
            jax.ShapeDtypeStruct((rows, boundary), BF16),
            jax.ShapeDtypeStruct((parts, boundary // parts, width), BF16),
        ),
        in_specs=[smem, smem, smem, vmem, vmem, vmem],
        out_specs=(vmem,) * 4,
        scratch_shapes=[pltpu.VMEM((rows // tile, (rows + boundary) // tile, tile, tile), F32)],
        compiler_params=pltpu.CompilerParams(vmem_limit_bytes=32 * 2**20),
        name="dense_tiles",
    )(tile_rows, tile_cols, tile_count, tile_values, chosen, features)


def cuts(width, parts):
    first = width // 3 * 2
    out = []
    for start, size in ((0, first), (first, width - first)):
        out.append((start, size, -(-size // (8 * parts)) * 8))
    return out


def step_kernel(npx, npy, *refs):
    (counts, own, rest, pick, box_x) = refs[:5]
    hbm = refs[5:11]
    got_h, got_g = refs[11:13]
    parts = npx * npy
    width = own.shape[0]
    pieces = cuts(width, parts)
    outs = refs[13:17]
    (
        features,
        w_two,
        out_grad,
        stale_g,
        w_one,
        stale_h,
        down,
        agg_own,
        hidden_grad,
        box_g,
        box_h,
        box_n,
        in_x,
        in_n,
        agg_one,
        hidden,
        pre_grad,
        agg_two,
    ) = refs[17:35]
    srcs = refs[35:39]
    scratch = refs[39:-5]
    load_sem, ex_send, ex_recv, red_send, red_recv = refs[-5:]
    slots = box_x.shape[1]
    px, py, me = positions(npx, npy)

    held = (features, w_two, out_grad, stale_g, w_one, stale_h)
    loads = [pltpu.make_async_copy(a, b, load_sem.at[i]) for i, (a, b) in enumerate(zip(hbm, held))]
    for copy in loads:
        copy.start()

    def fill(q, carry):
        box_n[q] = jnp.full(box_n.shape[1:], counts[0, q], jnp.int32)
        return carry

    lax.fori_loop(0, parts, fill, 0)
    entry_barrier(me, npx, npy)
    sem = lambda i, n: (ex_send.at[pl.ds(i, n)], ex_recv.at[pl.ds(i, n)])
    pairs_x = [(box_x, in_x), (box_n, in_n)]
    start_exchange(me, npx, npy, pairs_x, *sem(0, 2))

    block = width // 3

    def rows_of(i):
        return pl.ds(pl.multiple_of(i * block, 128), block)

    for copy in loads[:4]:
        copy.wait()

    def early(i, carry):
        r = rows_of(i)
        down[r, :] = dot(out_grad[r, :], w_two[...], 1, 1).astype(BF16)
        agg_own[r, :] = dot(own[r, :], features[...])
        return carry

    lax.fori_loop(0, 3, early, 0)
    back = dot(rest[...], down[...], 0, 0)
    box_g[...] = back.reshape(parts, slots, width).astype(BF16)

    def back_step(i, carry):
        r = rows_of(i)
        hidden_grad[r, :] = dot(own[:, r], down[...], 0, 0) + dot(pick[r, :], stale_g[...])
        return carry

    lax.fori_loop(0, 3, back_step, 0)
    for copy in loads[4:]:
        copy.wait()
    finish_exchange(parts, pairs_x, *sem(0, 2))
    pairs_g = [(box_g, got_g)]
    start_exchange(me, npx, npy, pairs_g, *sem(2, 1))

    arrived = in_x[...].astype(F32).reshape(parts * slots, width).astype(BF16)

    def layer_one(i, carry):
        r = rows_of(i)
        agg = (agg_own[r, :] + dot(rest[r, :], arrived)).astype(BF16)
        agg_one[r, :] = agg
        v = dot(agg, w_one[...])
        cdf = 0.5 * (1.0 + lax.erf(v * (1.0 / math.sqrt(2.0))))
        hidden[r, :] = (v * cdf).astype(BF16)
        slope = cdf + v * (jnp.exp(-0.5 * v * v) * (1.0 / math.sqrt(2.0 * math.pi)))
        pre_grad[r, :] = (hidden_grad[r, :] * slope).astype(BF16)
        return carry

    lax.fori_loop(0, 3, layer_one, 0)
    box = dot(pick[...], hidden[...], 0, 0)
    box_h[...] = box.reshape(parts, slots, width).astype(BF16)
    pairs_h = [(box_h, got_h)]
    start_exchange(me, npx, npy, pairs_h, *sem(3, 1))

    orders = reduce_orders(npx, npy)
    stages = len(orders[0])
    per = 2 * sum(size - 1 for _, _, size in orders[0]) // 2
    streams, at = [], 0
    for k in range(4):
        curs = scratch[at : at + stages - 1]
        recvs = scratch[at + stages - 1 : at + 2 * stages - 1]
        at += 2 * stages - 1
        sems = (red_send, red_recv, 2 * k * per)
        streams.append(Stream(orders[k % 2], parts, px, py, srcs[k], outs[k], curs, recvs, sems))

    def weight_grad(left, right, targets):
        for (start, size, height), target in zip(pieces, targets):
            for low in range(start, start + size, 128):
                part = dot(left[:, low : low + 128], right[...], 0, 0)
                c = (low - start) // height
                n = 128 // height
                target[c : c + n] = part.reshape(n, height, width).astype(BF16)
            full = size // height
            if full < parts:
                target[full:] = jnp.zeros((parts - full,) + target.shape[1:], BF16)

    weight_grad(agg_one, pre_grad, srcs[:2])
    for s in streams[:2]:
        s.scatter_start(0)

    slot = lax.broadcasted_iota(jnp.int32, (parts, slots, 128), 1)
    heard = slot < in_n[...]
    kept = []
    for low in range(0, width, 128):
        piece = stale_h[:, :, low : low + 128].astype(F32)
        kept.append(jnp.where(heard, piece, 0.0).reshape(parts * slots, 128).astype(BF16))
    kept = jnp.concatenate(kept, axis=1)

    def layer_two(i, carry):
        r = rows_of(i)
        agg_two[r, :] = (dot(own[r, :], hidden[...]) + dot(rest[r, :], kept)).astype(BF16)
        return carry

    lax.fori_loop(0, 3, layer_two, 0)
    for s in streams[:2]:
        s.scatter_finish(0)
        s.scatter_start(1)
    weight_grad(agg_two, out_grad, srcs[2:])
    for s in streams[2:]:
        s.scatter_start(0)
    for s in streams[2:]:
        s.scatter_finish(0)
        s.scatter_start(1)

    for stage in range(1, stages):
        for s in streams:
            s.scatter_finish(stage)
            if stage < stages - 1:
                s.scatter_start(stage + 1)
            else:
                s.gather_start(stage)
    for stage in range(stages - 1, -1, -1):
        for s in streams:
            s.gather_finish(stage)
            if stage > 0:
                s.gather_start(stage - 1)
    finish_exchange(parts, pairs_g, *sem(2, 1))
    finish_exchange(parts, pairs_h, *sem(3, 1))
    for s in streams:
        s.drain()


def step(npx, npy, counts, own, rest, pick, box_x, held):
    parts = npx * npy
    vmem = pl.BlockSpec(memory_space=pltpu.VMEM)
    smem = pl.BlockSpec(memory_space=pltpu.SMEM)
    hbm = pl.BlockSpec(memory_space=pl.ANY)
    width = own.shape[0]
    pieces = cuts(width, parts)
    orders = reduce_orders(npx, npy)
    heights = [p[2] for p in pieces] * 2
    chunked = [(parts, h, width) for h in heights]
    scratch = []
    for k in range(4):
        curs, recvs = scratch_for(orders[k % 2], parts, heights[k], width)
        scratch += curs + recvs
    count = 4 * 2 * sum(size - 1 for _, _, size in orders[0])
    dma = pltpu.SemaphoreType.DMA
    square = (width, width)
    box = box_x.shape
    mine = [pltpu.VMEM(a.shape, a.dtype) for a in held]
    mine += [pltpu.VMEM(square, BF16), pltpu.VMEM(square, F32), pltpu.VMEM(square, F32)]
    mine += [pltpu.VMEM(box, BF16), pltpu.VMEM(box, BF16)]
    mine += [pltpu.VMEM((parts, 1, 128), jnp.int32), pltpu.VMEM(box, BF16)]
    mine += [pltpu.VMEM((parts, 1, 128), jnp.int32)]
    mine += [pltpu.VMEM(square, BF16)] * 4
    mine += [pltpu.VMEM(c, BF16) for c in chunked]
    return pl.pallas_call(
        functools.partial(step_kernel, npx, npy),
        out_shape=tuple(jax.ShapeDtypeStruct(c, BF16) for c in [box, box] + chunked),
        in_specs=[smem] + [vmem] * 4 + [hbm] * 6,
        out_specs=(vmem,) * 6,
        scratch_shapes=mine + scratch + [dma((6,)), dma((4,)), dma((4,)), dma((count,)), dma((count,))],
        compiler_params=pltpu.CompilerParams(
            collective_id=0,
            has_side_effects=True,
            vmem_limit_bytes=min(36 + 26 * parts // 128, 62) * 2**20,
        ),
        name="graph_step",
    )(counts, own, rest, pick, box_x, *held)


def local(
    npx,
    npy,
    features,
    weight_one,
    weight_two,
    tile_values,
    tile_rows,
    tile_cols,
    tile_count,
    send_rows,
    send_count,
    stale_hidden,
    stale_grad,
    out_grad,
):
    parts = npx * npy
    rows_own, width = features.shape
    slots = send_rows.shape[2]
    slot_ids = jnp.arange(slots, dtype=jnp.int32)
    sent = (slot_ids[None, :] < send_count[0][:, None]).reshape(-1)
    chosen = jnp.where(sent, send_rows[0].reshape(-1), -1).reshape(1, -1)
    own, rest, pick, box_x = dense_tiles(
        tile_values, tile_rows, tile_cols, tile_count, chosen, features, parts
    )
    held = (
        features,
        weight_two,
        out_grad,
        stale_grad,
        weight_one,
        stale_hidden.reshape(parts, slots, width),
    )
    got_h, got_g, *sums = step(npx, npy, send_count, own, rest, pick, box_x, held)
    scale = 1.0 / math.sqrt(rows_own * parts)
    pieces = cuts(width, parts)

    def whole(blocks):
        flat = [a.reshape(-1, width)[: p[1]] for a, p in zip(blocks, pieces)]
        return jnp.concatenate(flat, axis=0).astype(F32) * scale

    got_g = got_g.reshape(-1, width)
    next_grad = jnp.where(sent[:, None], got_g, jnp.zeros_like(got_g))
    return got_h.reshape(-1, width), next_grad, whole(sums[:2]), whole(sums[2:])


def solution(mesh):
    in_specs = (
        P(("px", "py"), None),
        P(),
        P(),
        P(("px", "py"), None, None),
        P(("px", "py"), None),
        P(("px", "py"), None),
        P(("px", "py")),
        P(("px", "py"), None, None),
        P(("px", "py"), None),
        P(("px", "py"), None),
        P(("px", "py"), None),
        P(("px", "py"), None),
    )
    out_specs = (P(("px", "py"), None), P(("px", "py"), None), P(), P())
    body = functools.partial(local, mesh.shape["px"], mesh.shape["py"])
    return jax.shard_map(body, mesh=mesh, in_specs=in_specs, out_specs=out_specs, check_vma=False)
```

time: 119 us -> 84.8 us (0.71)
  matrix products: 29.2 us -> 0 us
  Pallas kernels: 78.5 us -> 68.6 us
  local copies, waits for them, and re-layouts: 3.29 us -> 10.1 us
  other arithmetic: 5.95 us -> 4.19 us
    dot_general x11 -> x0, matrix products: 29.2 us -> none  [dot(): lax.dot_general(a, b, (((ca,), (cb,)), ((), ())), preferred_element_type=...]
    pallas_call x2 -> x1, Pallas kernels: 77.5 us -> 67 us  [step(): pl.pallas_call(functools.partial(step_kernel, npx, npy), out_shape=tuple(...]
    unnamed x26 -> x24, local copies, waits for them, and re-layouts: 1.58 us -> 9.78 us
    mul x1, other arithmetic: 4.28 us -> 2.6 us  [whole(): return jnp.concatenate(flat, axis=0).astype(F32) * scale]
where the time goes in v1:
time: 84.8 us; the launch traced here: 84.2 us
  Pallas kernels  68.6 us (81%)
  local copies, waits for them, and re-layouts  10.1 us (12%)
  other arithmetic  4.19 us (5%)
  between operations  1.35 us (2%)
    pallas_call x1, Pallas kernels, step(): pl.pallas_call(functools.partial(step_kernel, npx, npy), out_shape=tuple(...  67 us
    unnamed x24, local copies, waits for them, and re-layouts  9.78 us
    mul x1, other arithmetic, whole(): return jnp.concatenate(flat, axis=0).astype(F32) * scale  2.6 us

profile of v1, /device:TPU:0, one launch (start us, length us, event | category | flops | bytes accessed | tf_op | source)
XLA Modules:
  0.0 84.2 jit_solution(584411087388148026)
XLA Ops:
  1.3 0.7 iota_compare_fusion
  2.0 0.1 lt.38
  2.1 0.1 lt.37
  2.2 0.8 copy.17
  3.0 0.1 reshape_squeeze.3
  3.1 0.0 copy-start
  3.1 1.3 %copy-done = bf16[768,768]{1,0:T(8,128)(2,1)S(1)} copy-done((bf16[768,768]{1,0:T(8,128)(2,1)S(1)}, bf16[768,768]{1,0:T(8,128)(2,1)}, u32[]{:S(2)}) %copy-start) | copy-done | bytes 1179672
  4.3 0.0 copy-start.5
  4.3 1.2 %copy-done.5 = bf16[32,128,128]{2,1,0:T(8,128)(2,1)S(1)} copy-done((bf16[32,128,128]{2,1,0:T(8,128)(2,1)S(1)}, bf16[32,128,128]{2,1,0:T(8,128)(2,1)}, u32[]{:S(2)}) %copy-start.5) | copy-done | bytes 1048600
  5.6 0.0 copy-start.9
  5.6 0.7 copy-done.9
  6.2 0.0 copy-start.10
  6.2 0.7 copy-done.10
  6.9 0.0 copy-start.1
  6.9 0.0 copy-start.6
  6.9 0.0 copy-start.7
  6.9 1.6 %dense_tiles.1 = (bf16[768,768]{1,0:T(8,128)(2,1)S(1)}, bf16[768,256]{1,0:T(8,128)(2,1)S(1)}, bf16[768,256]{1,0:T(8,128)(2,1)S(1)}, bf16[32,8,768]{2,1,0:T(8,128)(2,1)S(1)}) custom-call(s32[1,32]{1,0:T(1,128)S(1)} %copy-done.9, s32[1,32]{1,0:T(1,128)S(1)} %copy-done.10, s32[1]{0:T(128)S(6)} %copy.19.live, bf16[32,128,128]{2,1,0:T(8,128)(2,1)S(1)} %copy-done.5, ...), custom_call_target="tpu_custom_call" | custom-call | tf_op jit(solution)/shard_map/dense_tiles/pallas_call | solution.py:211
  8.5 0.0 copy-done.1
  8.5 0.0 copy-done.6
  8.5 0.0 copy-done.7
  8.5 0.0 copy-start.2
  8.5 1.3 %copy-done.2 = bf16[768,768]{1,0:T(8,128)(2,1)S(1)} copy-done((bf16[768,768]{1,0:T(8,128)(2,1)S(1)}, bf16[768,768]{1,0:T(8,128)(2,1)}, u32[]{:S(2)}) %copy-start.2) | copy-done | bytes 1179672
  9.8 0.0 copy-start.3
  9.8 1.3 %copy-done.3 = bf16[768,768]{1,0:T(8,128)(2,1)S(1)} copy-done((bf16[768,768]{1,0:T(8,128)(2,1)S(1)}, bf16[768,768]{1,0:T(8,128)(2,1)}, u32[]{:S(2)}) %copy-start.3) | copy-done | bytes 1179672
  11.1 0.0 copy-start.4
  11.1 1.3 %copy-done.4 = bf16[768,768]{1,0:T(8,128)(2,1)S(1)} copy-done((bf16[768,768]{1,0:T(8,128)(2,1)S(1)}, bf16[768,768]{1,0:T(8,128)(2,1)}, u32[]{:S(2)}) %copy-start.4) | copy-done | bytes 1179672
  12.3 0.0 copy-start.8
  12.3 0.7 copy-done.8
  13.0 67.0 %graph_step.1 = (bf16[32,8,768]{2,1,0:T(8,128)(2,1)S(1)}, bf16[32,8,768]{2,1,0:T(8,128)(2,1)S(1)}, bf16[32,16,768]{2,1,0:T(8,128)(2,1)S(1)}, bf16[32,8,768]{2,1,...) custom-call(s32[1,32]{1,0:T(1,128)S(1)} %copy-done.8, ...), custom_call_target="tpu_custom_call" | custom-call | tf_op jit(solution)/shard_map/graph_step/pallas_call | solution.py:426
  80.0 0.9 %bitcast_select_fusion = bf16[256,768]{1,0:T(8,128)(2,1)} fusion(bf16[32,8,768]{2,1,0:T(8,128)(2,1)S(1)} %get-tuple-element.19, pred[256]{0:T(512)(128)(4,1)S(1)} %lt.38), kind=kLoop, calls=%fused_computation.2 | loop fusion | flops 196608 | bytes 786688 | tf_op jit(solution)/shard_map/jit(_where)/select_n | solution.py:483
  80.9 2.6 %convert_multiply_fusion = (f32[768,768]{1,0:T(8,128)}, f32[768,768]{1,0:T(8,128)}) fusion(bf16[256,768]{1,0:T(8,128)(2,1)S(1)} %bitcast.13, bf16[512,768]{1,0:T(8,128)(2,1)S(1)} %bitcast.10, bf16[256,768]{1,0:T(8,128)(2,1)S(1)} %bitcast.12, bf16[512,768]{1,0:T(8,128)(2,1)S(1)} %bitcast.9), kind=kLoop, calls=%fused_computation | loop fusion | flops 5898240 | bytes 7077888 | tf_op jit(solution)/shard_map/mul | solution.py:480
  83.5 0.7 copy.20
  (1 shorter events, 0.0 us)
Async XLA Ops:
  3.1 1.3 %copy-start = (bf16[768,768]{1,0:T(8,128)(2,1)S(1)}, bf16[768,768]{1,0:T(8,128)(2,1)}, u32[]{:S(2)}) copy-start(bf16[768,768]{1,0:T(8,128)(2,1)} %refs_5_.1) | copy-start | bytes 3538948
  4.3 1.2 %copy-start.5 = (bf16[32,128,128]{2,1,0:T(8,128)(2,1)S(1)}, bf16[32,128,128]{2,1,0:T(8,128)(2,1)}, u32[]{:S(2)}) copy-start(bf16[32,128,128]{2,1,0:T(8,128)(2,1)} %tiles.1) | copy-start | bytes 3145732
  5.6 0.7 copy-start.9
  6.2 0.7 copy-start.10
  6.9 1.6 %copy-start.1 = (bf16[768,768]{1,0:T(8,128)(2,1)S(1)}, bf16[768,768]{1,0:T(8,128)(2,1)}, u32[]{:S(2)}) copy-start(bf16[768,768]{1,0:T(8,128)(2,1)} %refs_5_.1) | copy-start | bytes 3538948
  6.9 1.6 %copy-start.6 = (bf16[256,768]{1,0:T(8,128)(2,1)S(1)}, bf16[256,768]{1,0:T(8,128)(2,1)}, u32[]{:S(2)}) copy-start(bf16[256,768]{1,0:T(8,128)(2,1)} %refs_8_.1) | copy-start | bytes 1179652
  6.9 1.6 %copy-start.7 = (bf16[256,768]{1,0:T(8,128)(2,1)S(1)}, bf16[256,768]{1,0:T(8,128)(2,1)}, u32[]{:S(2)}) copy-start(bf16[256,768]{1,0:T(8,128)(2,1)} %param.21) | copy-start | bytes 1179652
  8.5 1.3 %copy-start.2 = (bf16[768,768]{1,0:T(8,128)(2,1)S(1)}, bf16[768,768]{1,0:T(8,128)(2,1)}, u32[]{:S(2)}) copy-start(bf16[768,768]{1,0:T(8,128)(2,1)} %refs_6_.1) | copy-start | bytes 3538948
  9.8 1.3 %copy-start.3 = (bf16[768,768]{1,0:T(8,128)(2,1)S(1)}, bf16[768,768]{1,0:T(8,128)(2,1)}, u32[]{:S(2)}) copy-start(bf16[768,768]{1,0:T(8,128)(2,1)} %refs_7_.1) | copy-start | bytes 3538948
  11.1 1.3 %copy-start.4 = (bf16[768,768]{1,0:T(8,128)(2,1)S(1)}, bf16[768,768]{1,0:T(8,128)(2,1)}, u32[]{:S(2)}) copy-start(bf16[768,768]{1,0:T(8,128)(2,1)} %refs_9_.1) | copy-start | bytes 3538948
  12.3 0.7 copy-start.8

commit v2 on v1

--- a/solution.py
+++ b/solution.py
@@ -402,7 +402,7 @@
     parts = npx * npy
     vmem = pl.BlockSpec(memory_space=pltpu.VMEM)
     smem = pl.BlockSpec(memory_space=pltpu.SMEM)
-    hbm = pl.BlockSpec(memory_space=pl.ANY)
+    hbm = pl.BlockSpec(memory_space=pltpu.HBM)
     width = own.shape[0]
     pieces = cuts(width, parts)
     orders = reduce_orders(npx, npy)
@@ -432,7 +432,7 @@
         compiler_params=pltpu.CompilerParams(
             collective_id=0,
             has_side_effects=True,
-            vmem_limit_bytes=min(36 + 26 * parts // 128, 62) * 2**20,
+            vmem_limit_bytes=min(50 + 8 * parts // 128, 62) * 2**20,
         ),
         name="graph_step",
     )(counts, own, rest, pick, box_x, *held)

time: 84.8 us -> 85.4 us (level)
  other arithmetic: 4.19 us -> 5.56 us
  local copies, waits for them, and re-layouts: 10.1 us -> 8.75 us
    mul x1, other arithmetic: 2.6 us -> 3.97 us  [whole(): return jnp.concatenate(flat, axis=0).astype(F32) * scale]
    unnamed x24 -> x18, local copies, waits for them, and re-layouts: 9.78 us -> 8.46 us
where the time goes in v2:
time: 85.4 us; the launch traced here: 85 us
  Pallas kernels  69.3 us (81%)
  local copies, waits for them, and re-layouts  8.75 us (10%)
  other arithmetic  5.56 us (7%)
  between operations  1.33 us (2%)
    pallas_call x1, Pallas kernels, step(): pl.pallas_call(functools.partial(step_kernel, npx, npy), out_shape=tuple(...  67.8 us
    unnamed x18, local copies, waits for them, and re-layouts  8.46 us
    mul x1, other arithmetic, whole(): return jnp.concatenate(flat, axis=0).astype(F32) * scale  3.97 us

profile of v2, /device:TPU:0, one launch (start us, length us, event | category | flops | bytes accessed | tf_op | source)
XLA Modules:
  0.0 85.0 jit_solution(10422687417131499202)
XLA Ops:
  1.3 0.7 iota_compare_fusion
  2.0 0.1 lt.38
  2.1 0.1 lt.37
  2.2 0.8 copy.17
  3.0 0.1 reshape_squeeze.3
  3.1 0.0 copy-start
  3.1 1.3 %copy-done = bf16[768,768]{1,0:T(8,128)(2,1)S(1)} copy-done((bf16[768,768]{1,0:T(8,128)(2,1)S(1)}, bf16[768,768]{1,0:T(8,128)(2,1)}, u32[]{:S(2)}) %copy-start) | copy-done | bytes 1179672
  4.3 0.0 copy-start.2
  4.3 1.2 %copy-done.2 = bf16[32,128,128]{2,1,0:T(8,128)(2,1)S(1)} copy-done((bf16[32,128,128]{2,1,0:T(8,128)(2,1)S(1)}, bf16[32,128,128]{2,1,0:T(8,128)(2,1)}, u32[]{:S(2)}) %copy-start.2) | copy-done | bytes 1048600
  5.6 0.0 copy-start.6
  5.6 0.7 copy-done.6
  6.2 0.0 copy-start.7
  6.2 0.7 copy-done.7
  6.9 1.5 %dense_tiles.1 = (bf16[768,768]{1,0:T(8,128)(2,1)S(1)}, bf16[768,256]{1,0:T(8,128)(2,1)S(1)}, bf16[768,256]{1,0:T(8,128)(2,1)S(1)}, bf16[32,8,768]{2,1,0:T(8,128)(2,1)S(1)}) custom-call(s32[1,32]{1,0:T(1,128)S(1)} %copy-done.6, s32[1,32]{1,0:T(1,128)S(1)} %copy-done.7, s32[1]{0:T(128)S(6)} %copy.19.live, bf16[32,128,128]{2,1,0:T(8,128)(2,1)S(1)} %copy-done.2, ...), custom_call_target="tpu_custom_call" | custom-call | tf_op jit(solution)/shard_map/dense_tiles/pallas_call | solution.py:211
  8.4 0.0 copy-start.1
  8.4 1.0 %copy-done.1 = bf16[768,768]{1,0:T(8,128)(2,1)} copy-done((bf16[768,768]{1,0:T(8,128)(2,1)}, bf16[768,768]{1,0:T(8,128)(2,1)S(1)}, u32[]{:S(2)}) %copy-start.1) | copy-done | bytes 1179672
  9.5 0.0 copy-start.3
  9.5 0.7 copy-done.3
  10.2 0.0 copy-start.4
  10.2 0.7 copy-done.4
  10.9 0.0 copy-start.5
  10.9 0.7 copy-done.5
  11.6 67.8 %graph_step.1 = (bf16[32,8,768]{2,1,0:T(8,128)(2,1)S(1)}, bf16[32,8,768]{2,1,0:T(8,128)(2,1)S(1)}, bf16[32,16,768]{2,1,0:T(8,128)(2,1)}, bf16[32,8,768]{2,1,0:T(...) custom-call(s32[1,32]{1,0:T(1,128)S(1)} %copy-done.5, bf16[768,768]{1,0:T(8,128)(2,1)} %copy-done.1, ...), custom_call_target="tpu_custom_call" | custom-call | tf_op jit(solution)/shard_map/graph_step/pallas_call | solution.py:426
  79.4 0.9 %bitcast_select_fusion = bf16[256,768]{1,0:T(8,128)(2,1)} fusion(bf16[32,8,768]{2,1,0:T(8,128)(2,1)S(1)} %get-tuple-element.19, pred[256]{0:T(512)(128)(4,1)S(1)} %lt.38), kind=kLoop, calls=%fused_computation.2 | loop fusion | flops 196608 | bytes 786688 | tf_op jit(solution)/shard_map/jit(_where)/select_n | solution.py:483
  80.2 4.0 %convert_multiply_fusion = (f32[768,768]{1,0:T(8,128)}, f32[768,768]{1,0:T(8,128)}) fusion(bf16[256,768]{1,0:T(8,128)(2,1)S(1)} %bitcast.10, bf16[512,768]{1,0:T(8,128)(2,1)} %bitcast.14, bf16[256,768]{1,0:T(8,128)(2,1)S(1)} %bitcast.9, bf16[512,768]{1,0:T(8,128)(2,1)} %bitcast.13), kind=kLoop, calls=%fused_computation | loop fusion | flops 5898240 | bytes 7077888 | tf_op jit(solution)/shard_map/mul | solution.py:480
  84.2 0.7 copy.20
  (1 shorter events, 0.0 us)
Async XLA Ops:
  3.1 1.3 %copy-start = (bf16[768,768]{1,0:T(8,128)(2,1)S(1)}, bf16[768,768]{1,0:T(8,128)(2,1)}, u32[]{:S(2)}) copy-start(bf16[768,768]{1,0:T(8,128)(2,1)} %refs_5_.1) | copy-start | bytes 3538948
  4.3 1.2 %copy-start.2 = (bf16[32,128,128]{2,1,0:T(8,128)(2,1)S(1)}, bf16[32,128,128]{2,1,0:T(8,128)(2,1)}, u32[]{:S(2)}) copy-start(bf16[32,128,128]{2,1,0:T(8,128)(2,1)} %tiles.1) | copy-start | bytes 3145732
  5.6 0.7 copy-start.6
  6.2 0.7 copy-start.7
  8.4 1.0 %copy-start.1 = (bf16[768,768]{1,0:T(8,128)(2,1)}, bf16[768,768]{1,0:T(8,128)(2,1)S(1)}, u32[]{:S(2)}) copy-start(bf16[768,768]{1,0:T(8,128)(2,1)S(1)} %get-tuple-element.14.refs_1_) | copy-start | bytes 3538948
  9.5 0.7 copy-start.3
  10.2 0.7 copy-start.4
  10.9 0.7 copy-start.5
